TPU v7x, 32 devices: a whole 2x2x4 slice. The times are simulated.
32 devices in a mesh: tm: 4 (over z), ent: 2 (over y), batch: 4 (over x, core).
Axes of the slice: x: 2, y: 2, z: 4, core: 2. Of those that a mesh axis runs over, the one named last changes fastest.
Arguments:
- init_state: float32 [4, 1024, 256], P('batch', 'ent'), may hold values from -6 to 6
- tiles: float32 [4, 4, 4, 512, 512], P('batch', 'tm', 'ent'), may hold values from -0.25 to 0.25
- dst_block: int32 [4, 4, 4], P('batch', 'tm', 'ent'), may hold values from 0 to 1
- rel_id: int32 [4, 4, 4], P('batch', 'tm', 'ent'), may hold values from 0 to 255
- cotangent: float32 [4, 4, 1024, 256], P('batch', 'tm', 'ent'), may hold values from -0.125 to 0.125
- rel_emb: float32 [256, 256], replicated, may hold values from -6 to 6
- w_neigh: float32 [256, 256], replicated, may hold values from -0.1875 to 0.1875
- w_self: float32 [256, 256], replicated, may hold values from -0.375 to 0.375
- w_gate: float32 [256, 256], replicated, may hold values from -0.375 to 0.375
- b_gate: float32 [256], replicated, may hold values from -2 to 2
Outputs:
- states: float32 [4, 4, 1024, 256], P('batch', 'tm', 'ent')
- grad_rel: float32 [256, 256], replicated
- grad_neigh: float32 [256, 256], replicated
- grad_self: float32 [256, 256], replicated
- grad_gate: float32 [256, 256], replicated
- grad_bias: float32 [256], replicated
All inputs are finite; a program needn't handle non-finite values.
Results may differ from a plain program's by a relative error of at most 0.00012.
Values sent between devices are 32-bit elements; how exact they have to be, the bound alone decides.
A program may use at most 64 MiB of HBM per device.

v0:
```python
import jax
import jax.numpy as jnp
from jax import lax
from jax.sharding import PartitionSpec as P

highest = lax.Precision.HIGHEST


def shifted(value, axis, steps):
    count = lax.axis_size(axis)
    first, last = (max(0, -steps), min(count, count - steps))
    return lax.ppermute(value, axis, [(source, source + steps) for source in range(first, last)])


def product(left, right):
    return jnp.dot(left, right, precision=highest)


def block_terms(current, tiles_t, rel_t, rel_emb):
    rows_sum = jnp.sum(tiles_t, axis=2)
    rel_pick = (rel_t[:, None] == jnp.arange(rel_emb.shape[0], dtype=jnp.int32)[None, :]).astype(
        jnp.float32
    )
    rel_rows = product(rel_pick, rel_emb)
    result = jnp.einsum("tij,jd->tid", tiles_t, current, precision=highest)
    return result + rows_sum[:, :, None] * rel_rows[:, None, :]


def dest_table(dst_t):
    count = lax.axis_size("ent")
    return (dst_t[:, None] == jnp.arange(count, dtype=jnp.int32)[None, :]).astype(jnp.float32)


def gru_forward(current, incoming, params):
    rel_emb, w_neigh, w_self, w_gate, b_gate = params
    update_gate = jax.nn.sigmoid(product(current, w_gate) + b_gate)
    candidate = jnp.tanh(product(incoming, w_neigh) + product(current, w_self))
    return (update_gate * candidate + (1.0 - update_gate) * current, update_gate, candidate)


def gru_backward(d_new, current, incoming, update_gate, candidate, params):
    rel_emb, w_neigh, w_self, w_gate, b_gate = params
    d_update = d_new * (candidate - current)
    d_cand = d_new * update_gate
    d_pre = d_cand * (1.0 - candidate * candidate)
    d_gate_in = d_update * update_gate * (1.0 - update_gate)
    d_prev = d_new * (1.0 - update_gate) + product(d_pre, w_self.T) + product(d_gate_in, w_gate.T)
    d_incoming = product(d_pre, w_neigh.T)
    dense_grads = (
        product(incoming.T, d_pre),
        product(current.T, d_pre),
        product(current.T, d_gate_in),
        jnp.sum(d_gate_in, axis=0),
    )
    return (d_prev, d_incoming, dense_grads)


def tile_backward(d_res, tiles_t, rel_t, rel_count):
    d_held = jnp.einsum("tij,tid->jd", tiles_t, d_res, precision=highest)
    rows_sum = jnp.sum(tiles_t, axis=2)
    per_tile = jnp.einsum("ti,tid->td", rows_sum, d_res, precision=highest)
    rel_pick = (rel_t[:, None] == jnp.arange(rel_count, dtype=jnp.int32)[None, :]).astype(
        jnp.float32
    )
    return (d_held, jnp.einsum("tr,td->rd", rel_pick, per_tile, precision=highest))


def natural_step(current, tiles_t, dst_t, rel_t, params):
    result = block_terms(current, tiles_t, rel_t, params[0])
    partial_value = jnp.einsum("tg,tid->gid", dest_table(dst_t), result, precision=highest)
    incoming = lax.psum_scatter(partial_value, "ent", scatter_dimension=0, tiled=True)[0]
    return (incoming,) + gru_forward(current, incoming, params)


def natural_spread(d_incoming, dst_t):
    gathered = lax.all_gather(d_incoming[None], "ent", axis=0, tiled=True)
    return jnp.einsum("tg,gid->tid", dest_table(dst_t), gathered, precision=highest)


def run_forward(begin_state, stacks, params, advance_fn):

    def advance(current, inputs):
        tiles_t, dst_t, rel_t = inputs
        incoming, new_state, update_gate, candidate = advance_fn(
            current, tiles_t, dst_t, rel_t, params
        )
        return (new_state, (current, incoming, update_gate, candidate, new_state))

    return lax.scan(advance, begin_state, stacks)


def run_backward(d_last, stored, stacks, targets, params, spread_fn):
    rel_emb = params[0]
    empty = (
        jnp.zeros_like(rel_emb),
        jnp.zeros_like(params[1]),
        jnp.zeros_like(params[2]),
        jnp.zeros_like(params[3]),
        jnp.zeros_like(params[4]),
    )

    def retreat(carry, inputs):
        d_state, weight_sums = carry
        (current, incoming, update_gate, candidate), (tiles_t, dst_t, rel_t), target_t = inputs
        d_new = d_state + target_t
        d_prev, d_incoming, dense_grads = gru_backward(
            d_new, current, incoming, update_gate, candidate, params
        )
        d_res = spread_fn(d_incoming, dst_t)
        d_held, d_rel = tile_backward(d_res, tiles_t, rel_t, rel_emb.shape[0])
        summed = (
            weight_sums[0] + d_rel,
            weight_sums[1] + dense_grads[0],
            weight_sums[2] + dense_grads[1],
            weight_sums[3] + dense_grads[2],
            weight_sums[4] + dense_grads[3],
        )
        return ((d_prev + d_held, summed), None)

    (d_first, weight_sums), unused = lax.scan(
        retreat, (d_last, empty), (stored, stacks, targets), reverse=True
    )
    return (d_first, weight_sums)


def on_device(
    init_state, tiles, dst_block, rel_id, cotangent, rel_emb, w_neigh, w_self, w_gate, b_gate
):
    params = (rel_emb, w_neigh, w_self, w_gate, b_gate)
    n_tm = lax.axis_size("tm")
    stacks = (tiles[0], dst_block[0], rel_id[0])
    targets = cotangent[0]
    is_first = lax.axis_index("tm") == 0
    begin_state = init_state[0]
    stored_all = None
    for round_index in range(n_tm):
        last_state, stored_all = run_forward(begin_state, stacks, params, natural_step)
        if round_index + 1 < n_tm:
            passed = shifted(last_state, "tm", 1)
            begin_state = jnp.where(is_first, init_state[0], passed)
    stored = stored_all[:4]
    d_last = jnp.zeros_like(init_state[0])
    weight_grads = None
    for round_index in range(n_tm):
        d_first, weight_grads = run_backward(
            d_last, stored, stacks, targets, params, natural_spread
        )
        if round_index + 1 < n_tm:
            d_last = shifted(d_first, "tm", -1)
    state_out = stored_all[4][None]
    totals = lax.psum(weight_grads, ("tm", "ent", "batch"))
    return (state_out, totals[0], totals[1], totals[2], totals[3], totals[4])


def solution(mesh):
    placed = (
        P("batch", "ent", None),
        P("batch", "tm", "ent", None, None),
        P("batch", "tm", "ent"),
        P("batch", "tm", "ent"),
        P("batch", "tm", "ent", None),
        P(),
        P(),
        P(),
        P(),
        P(),
    )
    return jax.shard_map(
        on_device,
        mesh=mesh,
        in_specs=placed,
        out_specs=(P("batch", "tm", "ent", None), P(), P(), P(), P(), P()),
        check_vma=False,
    )
```

profile of v0, /device:TPU:0, one launch (start us, length us, event | category | flops | bytes accessed | tf_op | source)
XLA Modules:
  0.0 520.5 jit_solution(6965761714206291700)
XLA Ops:
  7.2 2.0 reduce_sum.32
  9.4 2.9 fusion.12
  12.6 3.5 fusion.66
  18.9 21.7 %reduce-scatter.5.cloned.1.call-done = f32[1,512,256]{2,1,0:T(8,128)} async-done(((f32[2,512,256]{2,1,0:T(8,128)}), f32[1,512,256]{2,1,0:T(8,128)}) %reduce-scatter.5.cloned.1.call-update) | async-done | bytes 524304 | tf_op jit(solution)/shard_map/while/body/eval_jaxpr/reduce_scatter | solution.py:71
  40.6 1.6 fusion.82
  42.2 2.4 fusion.45
  44.7 4.3 collective-permute-start
  49.0 10.4 %collective-permute-done = f32[512,256]{1,0:T(8,128)} collective-permute-done((f32[512,256]{1,0:T(8,128)}, f32[512,256]{1,0:T(8,128)}, u32[]{:S(2)}, u32[]{:S(2)}) %collective-permute-start) | collective-permute-done | bytes 524320 | tf_op jit(solution)/shard_map/ppermute | solution.py:12
  60.2 4.5 fusion.10
  64.8 2.2 copy.28
  67.0 3.8 fusion.63
  71.9 2.4 fusion.42
  74.4 20.1 %reduce-scatter.7.cloned.1.call-done = f32[1,512,256]{2,1,0:T(8,128)} async-done(((f32[2,512,256]{2,1,0:T(8,128)}), f32[1,512,256]{2,1,0:T(8,128)}) %reduce-scatter.7.cloned.1.call-update) | async-done | bytes 524304 | tf_op jit(solution)/shard_map/while/body/eval_jaxpr/reduce_scatter | solution.py:71
  94.4 1.6 fusion.79
  96.1 2.0 fusion.38
  98.1 3.7 collective-permute-start.1
  101.8 10.7 %collective-permute-done.1 = f32[512,256]{1,0:T(8,128)S(1)} collective-permute-done((f32[512,256]{1,0:T(8,128)S(1)}, f32[512,256]{1,0:T(8,128)S(1)}, u32[]{:S(2)}, u32[]{:S(2)}) %collective-permute-start.1) | collective-permute-done | bytes 524320 | tf_op jit(solution)/shard_map/ppermute | solution.py:12
  113.4 4.5 fusion.8
  117.9 2.2 copy.29
  120.2 3.7 fusion.64
  126.5 20.1 %reduce-scatter.9.cloned.1.call-done = f32[1,512,256]{2,1,0:T(8,128)} async-done(((f32[2,512,256]{2,1,0:T(8,128)}), f32[1,512,256]{2,1,0:T(8,128)}) %reduce-scatter.9.cloned.1.call-update) | async-done | bytes 524304 | tf_op jit(solution)/shard_map/while/body/eval_jaxpr/reduce_scatter | solution.py:71
  146.6 1.7 fusion.76
  148.2 1.7 fusion.31
  149.9 3.7 collective-permute-start.2
  153.6 10.7 %collective-permute-done.2 = f32[512,256]{1,0:T(8,128)S(1)} collective-permute-done((f32[512,256]{1,0:T(8,128)S(1)}, f32[512,256]{1,0:T(8,128)S(1)}, u32[]{:S(2)}, u32[]{:S(2)}) %collective-permute-start.2) | collective-permute-done | bytes 524320 | tf_op jit(solution)/shard_map/ppermute | solution.py:12
  164.4 4.5 fusion.6
  168.9 2.2 copy.30
  171.2 3.7 fusion.65
  176.1 1.6 fusion.28
  177.7 19.9 %reduce-scatter.11.cloned.1.call-done = f32[1,512,256]{2,1,0:T(8,128)} async-done(((f32[2,512,256]{2,1,0:T(8,128)}), f32[1,512,256]{2,1,0:T(8,128)}) %reduce-scatter.11.cloned.1.call-update) | async-done | bytes 524304 | tf_op jit(solution)/shard_map/while/body/eval_jaxpr/reduce_scatter | solution.py:71
  197.6 1.7 fusion.73
  199.3 2.7 fusion.145
  202.8 1.4 fusion.113
  204.8 2.5 convolution_add_fusion.1
  207.2 18.5 %all-gather.9.cloned.1.call-done = f32[1024,256]{1,0:T(8,128)} async-done(((f32[512,256]{1,0:T(8,128)}), f32[1024,256]{1,0:T(8,128)}) %all-gather.9.cloned.1.call-update) | async-done | bytes 1048592 | tf_op jit(solution)/shard_map/while/body/eval_jaxpr/all_gather | solution.py:76
  225.7 4.5 fusion.61
  230.2 3.4 fusion.14
  234.4 1.4 collective-permute-start.3
  235.8 14.1 %collective-permute-done.3 = f32[512,256]{1,0:T(8,128)S(1)} collective-permute-done((f32[512,256]{1,0:T(8,128)S(1)}, f32[512,256]{1,0:T(8,128)S(1)}, u32[]{:S(2)}, u32[]{:S(2)}) %collective-permute-start.3) | collective-permute-done | bytes 524320 | tf_op jit(solution)/shard_map/ppermute | solution.py:12
  251.5 1.4 fusion.147
  253.2 2.4 fusion.146
  255.6 17.8 %all-gather.11.cloned.1.call-done = f32[1024,256]{1,0:T(8,128)} async-done(((f32[512,256]{1,0:T(8,128)}), f32[1024,256]{1,0:T(8,128)}) %all-gather.11.cloned.1.call-update) | async-done | bytes 1048592 | tf_op jit(solution)/shard_map/while/body/eval_jaxpr/all_gather | solution.py:76
  273.5 4.5 fusion.59
  278.0 3.4 fusion.17
  282.3 1.4 collective-permute-start.4
  283.7 14.1 %collective-permute-done.4 = f32[512,256]{1,0:T(8,128)S(1)} collective-permute-done((f32[512,256]{1,0:T(8,128)S(1)}, f32[512,256]{1,0:T(8,128)S(1)}, u32[]{:S(2)}, u32[]{:S(2)}) %collective-permute-start.4) | collective-permute-done | bytes 524320 | tf_op jit(solution)/shard_map/ppermute | solution.py:12
  299.4 1.4 fusion.149
  301.1 2.4 fusion.148
  303.5 17.8 %all-gather.13.cloned.1.call-done = f32[1024,256]{1,0:T(8,128)} async-done(((f32[512,256]{1,0:T(8,128)}), f32[1024,256]{1,0:T(8,128)}) %all-gather.13.cloned.1.call-update) | async-done | bytes 1048592 | tf_op jit(solution)/shard_map/while/body/eval_jaxpr/all_gather | solution.py:76
  321.3 4.5 fusion.57
  325.9 3.4 fusion.20
  330.2 1.4 collective-permute-start.5
  331.6 14.1 %collective-permute-done.5 = f32[512,256]{1,0:T(8,128)S(1)} collective-permute-done((f32[512,256]{1,0:T(8,128)S(1)}, f32[512,256]{1,0:T(8,128)S(1)}, u32[]{:S(2)}, u32[]{:S(2)}) %collective-permute-start.5) | collective-permute-done | bytes 524320 | tf_op jit(solution)/shard_map/ppermute | solution.py:12
  348.6 1.7 fusion.151
  350.3 1.7 fusion.152
  352.0 1.7 fusion.71
  353.8 15.1 %all-gather.15.cloned.1.call-done = f32[1024,256]{1,0:T(8,128)} async-done(((f32[512,256]{1,0:T(8,128)}), f32[1024,256]{1,0:T(8,128)}) %all-gather.15.cloned.1.call-update) | async-done | bytes 1048592 | tf_op jit(solution)/shard_map/while/body/eval_jaxpr/all_gather | solution.py:76
  368.8 4.5 fusion.55
  375.1 39.7 %psum.39 = f32[256]{0:T(256)} all-reduce(f32[256]{0:T(256)S(1)} %get-tuple-element.207), channel_id=1, replica_groups=mesh['tm'=4,'ent'=2,'batch'=4] {'tm','ent','batch'}, use_global_device_ids=true, to_apply=%region_10.11 | all-reduce | flops 256 | bytes 2048 | tf_op jit(solution)/shard_map/psum | solution.py:151
  414.8 92.3 %all-reduce.3.cloned.1.call-done = (f32[256,256]{1,0:T(8,128)}, f32[256,256]{1,0:T(8,128)}, f32[256,256]{1,0:T(8,128)}, f32[256,256]{1,0:T(8,128)}) async-done(((f32[256,256]{1,0:T(8,128)}, f32[256,256]{1,0:T(8,128)}, f32[256,256]{1,0:T(8,128)}, f32[256,256]{1,0:T(8,128)}), (f32[256,256]{1,0:T(8,128)}, f32[256,256]{1,0:T(8,128)}, f32[256,256]{1,0:T(8,128)}, ...) | async-done | bytes 1048592 | tf_op jit(solution)/shard_map/psum | solution.py:151
  507.1 1.7 copy.75
  508.7 1.7 copy.76
  510.4 1.7 copy.77
  512.1 1.7 copy.78
  (126 shorter events, 21.8 us)
Async XLA Ops:
  7.2 35.0 %copy-start = (f32[256,256]{1,0:T(8,128)S(1)}, f32[256,256]{1,0:T(8,128)}, u32[]{:S(2)}) copy-start(f32[256,256]{1,0:T(8,128)} %param.17) | copy-start | bytes 786436
  7.2 2.3 copy-start.1
  7.2 33.4 %reduce-scatter.5.cloned.1.call-start = ((), (), s32[]{:S(2)}) async-start(), calls=%async_computation.4 | async-start | bytes 1572864 | tf_op jit(solution)/shard_map/while/body/eval_jaxpr/reduce_scatter | solution.py:71
  9.2 3.2 copy-start.37
  9.2 3.2 copy-start.42
  9.2 3.4 copy-start.41
  9.4 3.1 copy-start.38
  16.1 1.2 copy-start.14
  16.2 1.4 copy-start.24
  16.2 1.3 copy-start.43
  17.3 23.3 %copy-start.9 = (f32[256,256]{1,0:T(8,128)S(1)}, f32[256,256]{1,0:T(8,128)}, u32[]{:S(2)}) copy-start(f32[256,256]{1,0:T(8,128)} %param.16) | copy-start | bytes 786436
  17.3 77.1 %reduce-scatter.7.cloned.1.call-start = ((), (), s32[]{:S(2)}) async-start(), calls=%async_computation.5 | async-start | bytes 1572864 | tf_op jit(solution)/shard_map/while/body/eval_jaxpr/reduce_scatter | solution.py:71
  44.7 14.7 %collective-permute-start = (f32[512,256]{1,0:T(8,128)}, f32[512,256]{1,0:T(8,128)}, u32[]{:S(2)}, u32[]{:S(2)}) collective-permute-start(f32[512,256]{1,0:T(8,128)} %fusion.45), channel_id=1, source_target_pairs={{0,8},{8,16},{16,24},{1,9},{9,17},{17,25},{2,10},{10,18},{18,26},{... | collective-permute-start | bytes 1572872 | tf_op jit(solution)/shard_map/ppermute | solution.py:12
  59.5 0.8 copy-start.21
  71.9 74.7 %reduce-scatter.9.cloned.1.call-start = ((), (), s32[]{:S(2)}) async-start(), calls=%async_computation.6 | async-start | bytes 1572864 | tf_op jit(solution)/shard_map/while/body/eval_jaxpr/reduce_scatter | solution.py:71
  98.1 14.4 %collective-permute-start.1 = (f32[512,256]{1,0:T(8,128)S(1)}, f32[512,256]{1,0:T(8,128)S(1)}, u32[]{:S(2)}, u32[]{:S(2)}) collective-permute-start(f32[512,256]{1,0:T(8,128)S(1)} %fusion.38), channel_id=1, source_target_pairs={{0,8},{8,16},{16,24},{1,9},{9,17},{17,25},{2,10},{10,18},{18,26},{... | collective-permute-start | bytes 1572872 | tf_op jit(solution)/shard_map/ppermute | solution.py:12
  112.6 0.8 copy-start.22
  113.4 6.8 %copy-start.39 = (f32[2,512]{0,1:T(8,128)S(1)}, f32[2,512]{0,1:T(8,128)}, u32[]{:S(2)}) copy-start(f32[2,512]{0,1:T(8,128)} %copy-done.38) | copy-start | bytes 12292
  123.9 1.2 copy-start.23
  125.0 72.5 %reduce-scatter.11.cloned.1.call-start = ((), (), s32[]{:S(2)}) async-start(), calls=%async_computation.7 | async-start | bytes 1572864 | tf_op jit(solution)/shard_map/while/body/eval_jaxpr/reduce_scatter | solution.py:71
  146.6 17.8 %copy-start.15 = (f32[1,512,256]{2,1,0:T(8,128)S(1)}, f32[1,512,256]{2,1,0:T(8,128)}, u32[]{:S(2)}) copy-start(f32[1,512,256]{2,1,0:T(8,128)} %param.10) | copy-start | bytes 1572868
  149.9 14.4 %collective-permute-start.2 = (f32[512,256]{1,0:T(8,128)S(1)}, f32[512,256]{1,0:T(8,128)S(1)}, u32[]{:S(2)}, u32[]{:S(2)}) collective-permute-start(f32[512,256]{1,0:T(8,128)S(1)} %fusion.31), channel_id=1, source_target_pairs={{0,8},{8,16},{16,24},{1,9},{9,17},{17,25},{2,10},{10,18},{18,26},{... | collective-permute-start | bytes 1572872 | tf_op jit(solution)/shard_map/ppermute | solution.py:12
  164.4 11.7 %copy-start.3 = (f32[512,256]{1,0:T(8,128)}, f32[512,256]{1,0:T(8,128)S(1)}, u32[]{:S(2)}) copy-start(f32[512,256]{1,0:T(8,128)S(1)} %bitcast_select_fusion.2) | copy-start | bytes 1572868
  164.4 6.8 %copy-start.40 = (f32[2,512]{0,1:T(8,128)S(1)}, f32[2,512]{0,1:T(8,128)}, u32[]{:S(2)}) copy-start(f32[2,512]{0,1:T(8,128)} %copy-done.38) | copy-start | bytes 12292
  176.0 49.6 %all-gather.9.cloned.1.call-start = ((), (), s32[]{:S(2)}) async-start(), calls=%async_computation.8 | async-start | bytes 1572864 | tf_op jit(solution)/shard_map/while/body/eval_jaxpr/all_gather | solution.py:76
  177.7 25.1 %copy-start.2 = (f32[1,1,512,256]{3,2,1,0:T(8,128)S(1)}, f32[1,1,512,256]{3,2,1,0:T(8,128)}, u32[]{:S(2)}) copy-start(f32[1,1,512,256]{3,2,1,0:T(8,128)} %param.14) | copy-start | bytes 1572868
  197.6 5.3 %copy-start.10 = (f32[256,256]{1,0:T(8,128)S(1)}, f32[256,256]{1,0:T(8,128)}, u32[]{:S(2)}) copy-start(f32[256,256]{1,0:T(8,128)} %param.16) | copy-start | bytes 786436
  202.0 0.8 copy-start.5
  204.2 69.2 %all-gather.11.cloned.1.call-start = ((), (), s32[]{:S(2)}) async-start(), calls=%async_computation.9 | async-start | bytes 1572864 | tf_op jit(solution)/shard_map/while/body/eval_jaxpr/all_gather | solution.py:76
  230.2 3.5 copy-start.16
  230.2 3.5 copy-start.25
  230.2 3.5 copy-start.36
  233.7 16.3 %copy-start.6 = (f32[512,256]{1,0:T(8,128)S(1)}, f32[512,256]{1,0:T(8,128)}, u32[]{:S(2)}) copy-start(f32[512,256]{1,0:T(8,128)} %copy-done.5) | copy-start | bytes 1572868
  234.4 17.1 %copy-start.11 = (f32[256,256]{1,0:T(8,128)S(1)}, f32[256,256]{1,0:T(8,128)}, u32[]{:S(2)}) copy-start(f32[256,256]{1,0:T(8,128)} %param.16) | copy-start | bytes 786436
  234.4 15.5 %collective-permute-start.3 = (f32[512,256]{1,0:T(8,128)S(1)}, f32[512,256]{1,0:T(8,128)S(1)}, u32[]{:S(2)}, u32[]{:S(2)}) collective-permute-start(f32[512,256]{1,0:T(8,128)S(1)} %fusion.23), channel_id=1, source_target_pairs={{8,0},{16,8},{24,16},{9,1},{17,9},{25,17},{10,2},{18,10},{26,18},{... | collective-permute-start | bytes 1572872 | tf_op jit(solution)/shard_map/ppermute | solution.py:12
  249.9 0.8 copy-start.28
  250.7 0.8 copy-start.19
  253.0 68.4 %all-gather.13.cloned.1.call-start = ((), (), s32[]{:S(2)}) async-start(), calls=%async_computation.10 | async-start | bytes 1572864 | tf_op jit(solution)/shard_map/while/body/eval_jaxpr/all_gather | solution.py:76
  277.9 3.5 copy-start.17
  278.0 3.5 copy-start.26
  278.0 3.5 copy-start.29
  278.0 3.5 copy-start.33
  281.5 16.3 %copy-start.7 = (f32[512,256]{1,0:T(8,128)S(1)}, f32[512,256]{1,0:T(8,128)}, u32[]{:S(2)}) copy-start(f32[512,256]{1,0:T(8,128)} %copy-done.5) | copy-start | bytes 1572868
  282.2 17.1 %copy-start.12 = (f32[256,256]{1,0:T(8,128)S(1)}, f32[256,256]{1,0:T(8,128)}, u32[]{:S(2)}) copy-start(f32[256,256]{1,0:T(8,128)} %param.16) | copy-start | bytes 786436
  282.3 15.5 %collective-permute-start.4 = (f32[512,256]{1,0:T(8,128)S(1)}, f32[512,256]{1,0:T(8,128)S(1)}, u32[]{:S(2)}, u32[]{:S(2)}) collective-permute-start(f32[512,256]{1,0:T(8,128)S(1)} %add_add_fusion.1), channel_id=1, source_target_pairs={{8,0},{16,8},{24,16},{9,1},{17,9},{25,17},{10,2},{18,10},{26,18},{... | collective-permute-start | bytes 1572872 | tf_op jit(solution)/shard_map/ppermute | solution.py:12
  297.8 0.8 copy-start.30
  298.6 0.8 copy-start.20
  300.8 68.0 %all-gather.15.cloned.1.call-start = ((), (), s32[]{:S(2)}) async-start(), calls=%async_computation.11 | async-start | bytes 1572864 | tf_op jit(solution)/shard_map/while/body/eval_jaxpr/all_gather | solution.py:76
  325.8 3.5 copy-start.18
  325.8 3.5 copy-start.27
  325.8 3.5 copy-start.31
  325.9 3.5 copy-start.34
  329.4 16.3 %copy-start.4 = (f32[512,256]{1,0:T(8,128)S(1)}, f32[512,256]{1,0:T(8,128)}, u32[]{:S(2)}) copy-start(f32[512,256]{1,0:T(8,128)} %copy-done.3) | copy-start | bytes 1572868
  329.4 16.3 %copy-start.8 = (f32[512,256]{1,0:T(8,128)S(1)}, f32[512,256]{1,0:T(8,128)}, u32[]{:S(2)}) copy-start(f32[512,256]{1,0:T(8,128)} %copy-done.5) | copy-start | bytes 1572868
  330.1 16.7 %copy-start.13 = (f32[256,256]{1,0:T(8,128)S(1)}, f32[256,256]{1,0:T(8,128)}, u32[]{:S(2)}) copy-start(f32[256,256]{1,0:T(8,128)} %param.16) | copy-start | bytes 786436
  330.2 15.5 %collective-permute-start.5 = (f32[512,256]{1,0:T(8,128)S(1)}, f32[512,256]{1,0:T(8,128)S(1)}, u32[]{:S(2)}, u32[]{:S(2)}) collective-permute-start(f32[512,256]{1,0:T(8,128)S(1)} %add_add_fusion), channel_id=1, source_target_pairs={{8,0},{16,8},{24,16},{9,1},{17,9},{25,17},{10,2},{18,10},{26,18},{... | collective-permute-start | bytes 1572872 | tf_op jit(solution)/shard_map/ppermute | solution.py:12
  346.9 3.5 copy-start.32
  346.9 5.2 copy-start.35
  348.3 158.7 %all-reduce.3.cloned.1.call-start = ((), (), s32[]{:S(2)}) async-start(), calls=%async_computation.12 | async-start | bytes 2097152 | tf_op jit(solution)/shard_map/psum | solution.py:151
Sparse Core Ops, SparseCore 0:
  17.4 23.1 reduce-scatter.4
  72.0 22.3 reduce-scatter.6
  125.1 21.3 reduce-scatter.8
  176.2 21.3 reduce-scatter.10
  204.4 21.2 all-gather.8
  253.1 20.3 all-gather.10
  300.9 20.3 all-gather.12
  348.4 20.3 all-gather.14
  375.2 131.8 all-reduce.2
where the time goes:
time: 527 us; the launch traced here: 521 us
  waiting for transfers between devices  317 us (60%)
  matrix products  104 us (20%)
  blocking collectives  39.7 us (8%)
  local copies, waits for them, and re-layouts  23.6 us (4%)
  starting transfers between devices  17.4 us (3%)
  between operations  14.8 us (3%)
    psum x1, waiting for transfers between devices, on_device(): totals = lax.psum(weight_grads, ('tm', 'ent', 'batch'))  92.3 us
    reduce_scatter x4, waiting for transfers between devices, natural_step(): lax.psum_scatter(partial_value, 'ent', scatter_dimension=0, tiled=True)[0]  81.7 us
    ppermute x6, waiting for transfers between devices, shifted(): lax.ppermute(value, axis, [(source, source + steps) for source in range(f...  74.1 us
    all_gather x4, waiting for transfers between devices, natural_spread(): gathered = lax.all_gather(d_incoming[None], 'ent', axis=0, tiled=True)  69.2 us
    dot_general x26, matrix products, product(): return jnp.dot(left, right, precision=highest)  42.8 us
    psum x1, blocking collectives, on_device(): totals = lax.psum(weight_grads, ('tm', 'ent', 'batch'))  39.7 us
    dot_general x4, matrix products, natural_spread(): jnp.einsum('tg,gid->tid', dest_table(dst_t), gathered, precision=highest)  17.9 us
    dot_general x4, matrix products, block_terms(): result = jnp.einsum('tij,jd->tid', tiles_t, current, precision=highest)  16.5 us
  transfers between devices with their start and end apart: 15, of which 15 were waited for; matrix products, arithmetic and copies ran while one was open for 4% of the time, Pallas kernels for 0%

commit v1 on v0

--- a/solution.py
+++ b/solution.py
@@ -148,7 +148,9 @@
         if round_index + 1 < n_tm:
             d_last = shifted(d_first, "tm", -1)
     state_out = stored_all[4][None]
-    totals = lax.psum(weight_grads, ("tm", "ent", "batch"))
+    totals = weight_grads
+    for s in (("ent", "batch"), "tm"):
+        totals = jax.lax.psum(totals, s)
     return (state_out, totals[0], totals[1], totals[2], totals[3], totals[4])
 
 

time: 527 us -> 506 us (0.960)
  blocking collectives: 39.7 us -> 24.5 us
    psum x1 -> x2, blocking collectives: 39.7 us -> 24.5 us  [on_device(): totals = jax.lax.psum(totals, s)]
    psum x1 -> x2, waiting for transfers between devices: 92.3 us -> 86.5 us  [on_device(): totals = jax.lax.psum(totals, s)]
  transfers between devices with their start and end apart: 15 -> 16, of which waited for: 15 -> 16; matrix products, arithmetic and copies ran while one was open for 4% -> 4% of each run, Pallas kernels for 0% -> 0%
where the time goes in v1:
time: 506 us; the launch traced here: 500 us
  waiting for transfers between devices  312 us (62%)
  matrix products  104 us (21%)
  blocking collectives  24.5 us (5%)
  local copies, waits for them, and re-layouts  23.7 us (5%)
  starting transfers between devices  17.5 us (3%)
  between operations  15.1 us (3%)
    psum x2, waiting for transfers between devices, on_device(): totals = jax.lax.psum(totals, s)  86.5 us
    reduce_scatter x4, waiting for transfers between devices, natural_step(): lax.psum_scatter(partial_value, 'ent', scatter_dimension=0, tiled=True)[0]  81.7 us
    ppermute x6, waiting for transfers between devices, shifted(): lax.ppermute(value, axis, [(source, source + steps) for source in range(f...  74.1 us
    all_gather x4, waiting for transfers between devices, natural_spread(): gathered = lax.all_gather(d_incoming[None], 'ent', axis=0, tiled=True)  69.2 us
    dot_general x26, matrix products, product(): return jnp.dot(left, right, precision=highest)  42.6 us
    psum x2, blocking collectives, on_device(): totals = jax.lax.psum(totals, s)  24.5 us
    dot_general x4, matrix products, natural_spread(): jnp.einsum('tg,gid->tid', dest_table(dst_t), gathered, precision=highest)  17.9 us
    dot_general x4, matrix products, block_terms(): result = jnp.einsum('tij,jd->tid', tiles_t, current, precision=highest)  16.5 us
  transfers between devices with their start and end apart: 16, of which 16 were waited for; matrix products, arithmetic and copies ran while one was open for 4% of the time, Pallas kernels for 0%

profile of v1, /device:TPU:0, one launch (start us, length us, event | category | flops | bytes accessed | tf_op | source)
XLA Modules:
  0.0 499.9 jit_solution(17315615349145521134)
XLA Ops:
  7.2 2.0 reduce_sum.32
  9.4 2.9 fusion.12
  12.6 3.5 fusion.66
  18.9 21.6 %reduce-scatter.5.cloned.1.call-done = f32[1,512,256]{2,1,0:T(8,128)} async-done(((f32[2,512,256]{2,1,0:T(8,128)}), f32[1,512,256]{2,1,0:T(8,128)}) %reduce-scatter.5.cloned.1.call-update) | async-done | bytes 524304 | tf_op jit(solution)/shard_map/while/body/eval_jaxpr/reduce_scatter | solution.py:71
  40.6 1.6 fusion.82
  42.2 2.4 fusion.45
  44.7 4.4 collective-permute-start
  49.0 10.3 %collective-permute-done = f32[512,256]{1,0:T(8,128)} collective-permute-done((f32[512,256]{1,0:T(8,128)}, f32[512,256]{1,0:T(8,128)}, u32[]{:S(2)}, u32[]{:S(2)}) %collective-permute-start) | collective-permute-done | bytes 524320 | tf_op jit(solution)/shard_map/ppermute | solution.py:12
  60.2 4.5 fusion.10
  64.7 2.3 copy.28
  67.0 3.8 fusion.63
  71.9 2.5 fusion.42
  74.4 20.0 %reduce-scatter.7.cloned.1.call-done = f32[1,512,256]{2,1,0:T(8,128)} async-done(((f32[2,512,256]{2,1,0:T(8,128)}), f32[1,512,256]{2,1,0:T(8,128)}) %reduce-scatter.7.cloned.1.call-update) | async-done | bytes 524304 | tf_op jit(solution)/shard_map/while/body/eval_jaxpr/reduce_scatter | solution.py:71
  94.4 1.6 fusion.79
  96.1 2.0 fusion.38
  98.0 3.7 collective-permute-start.1
  101.7 10.7 %collective-permute-done.1 = f32[512,256]{1,0:T(8,128)S(1)} collective-permute-done((f32[512,256]{1,0:T(8,128)S(1)}, f32[512,256]{1,0:T(8,128)S(1)}, u32[]{:S(2)}, u32[]{:S(2)}) %collective-permute-start.1) | collective-permute-done | bytes 524320 | tf_op jit(solution)/shard_map/ppermute | solution.py:12
  113.3 4.5 fusion.8
  117.8 2.3 copy.29
  120.1 3.7 fusion.64
  126.4 20.1 %reduce-scatter.9.cloned.1.call-done = f32[1,512,256]{2,1,0:T(8,128)} async-done(((f32[2,512,256]{2,1,0:T(8,128)}), f32[1,512,256]{2,1,0:T(8,128)}) %reduce-scatter.9.cloned.1.call-update) | async-done | bytes 524304 | tf_op jit(solution)/shard_map/while/body/eval_jaxpr/reduce_scatter | solution.py:71
  146.5 1.7 fusion.76
  148.1 1.6 fusion.31
  149.8 3.7 collective-permute-start.2
  153.5 10.7 %collective-permute-done.2 = f32[512,256]{1,0:T(8,128)S(1)} collective-permute-done((f32[512,256]{1,0:T(8,128)S(1)}, f32[512,256]{1,0:T(8,128)S(1)}, u32[]{:S(2)}, u32[]{:S(2)}) %collective-permute-start.2) | collective-permute-done | bytes 524320 | tf_op jit(solution)/shard_map/ppermute | solution.py:12
  164.3 4.5 fusion.6
  168.8 2.3 copy.30
  171.1 3.7 fusion.65
  176.0 1.6 fusion.28
  177.6 19.9 %reduce-scatter.11.cloned.1.call-done = f32[1,512,256]{2,1,0:T(8,128)} async-done(((f32[2,512,256]{2,1,0:T(8,128)}), f32[1,512,256]{2,1,0:T(8,128)}) %reduce-scatter.11.cloned.1.call-update) | async-done | bytes 524304 | tf_op jit(solution)/shard_map/while/body/eval_jaxpr/reduce_scatter | solution.py:71
  197.5 1.7 fusion.73
  199.2 2.6 fusion.145
  202.6 1.4 fusion.113
  204.6 2.5 convolution_add_fusion.1
  207.1 18.5 %all-gather.9.cloned.1.call-done = f32[1024,256]{1,0:T(8,128)} async-done(((f32[512,256]{1,0:T(8,128)}), f32[1024,256]{1,0:T(8,128)}) %all-gather.9.cloned.1.call-update) | async-done | bytes 1048592 | tf_op jit(solution)/shard_map/while/body/eval_jaxpr/all_gather | solution.py:76
  225.5 4.5 fusion.61
  230.0 3.4 fusion.14
  234.2 1.4 collective-permute-start.3
  235.7 14.1 %collective-permute-done.3 = f32[512,256]{1,0:T(8,128)S(1)} collective-permute-done((f32[512,256]{1,0:T(8,128)S(1)}, f32[512,256]{1,0:T(8,128)S(1)}, u32[]{:S(2)}, u32[]{:S(2)}) %collective-permute-start.3) | collective-permute-done | bytes 524320 | tf_op jit(solution)/shard_map/ppermute | solution.py:12
  253.0 2.4 fusion.146
  255.5 17.9 %all-gather.11.cloned.1.call-done = f32[1024,256]{1,0:T(8,128)} async-done(((f32[512,256]{1,0:T(8,128)}), f32[1024,256]{1,0:T(8,128)}) %all-gather.11.cloned.1.call-update) | async-done | bytes 1048592 | tf_op jit(solution)/shard_map/while/body/eval_jaxpr/all_gather | solution.py:76
  273.3 4.5 fusion.59
  277.9 3.4 fusion.17
  282.1 1.4 collective-permute-start.4
  283.6 14.1 %collective-permute-done.4 = f32[512,256]{1,0:T(8,128)S(1)} collective-permute-done((f32[512,256]{1,0:T(8,128)S(1)}, f32[512,256]{1,0:T(8,128)S(1)}, u32[]{:S(2)}, u32[]{:S(2)}) %collective-permute-start.4) | collective-permute-done | bytes 524320 | tf_op jit(solution)/shard_map/ppermute | solution.py:12
  301.0 2.4 fusion.148
  303.4 17.8 %all-gather.13.cloned.1.call-done = f32[1024,256]{1,0:T(8,128)} async-done(((f32[512,256]{1,0:T(8,128)}), f32[1024,256]{1,0:T(8,128)}) %all-gather.13.cloned.1.call-update) | async-done | bytes 1048592 | tf_op jit(solution)/shard_map/while/body/eval_jaxpr/all_gather | solution.py:76
  321.2 4.5 fusion.57
  325.8 3.4 fusion.20
  330.0 1.4 collective-permute-start.5
  331.5 14.1 %collective-permute-done.5 = f32[512,256]{1,0:T(8,128)S(1)} collective-permute-done((f32[512,256]{1,0:T(8,128)S(1)}, f32[512,256]{1,0:T(8,128)S(1)}, u32[]{:S(2)}, u32[]{:S(2)}) %collective-permute-start.5) | collective-permute-done | bytes 524320 | tf_op jit(solution)/shard_map/ppermute | solution.py:12
  348.5 1.7 fusion.151
  350.2 1.7 fusion.152
  351.9 1.7 fusion.71
  353.7 15.1 %all-gather.15.cloned.1.call-done = f32[1024,256]{1,0:T(8,128)} async-done(((f32[512,256]{1,0:T(8,128)}), f32[1024,256]{1,0:T(8,128)}) %all-gather.15.cloned.1.call-update) | async-done | bytes 1048592 | tf_op jit(solution)/shard_map/while/body/eval_jaxpr/all_gather | solution.py:76
  368.7 4.5 fusion.55
  375.0 57.1 %all-reduce.5.cloned.1.call-done = (f32[256,256]{1,0:T(8,128)}, f32[256,256]{1,0:T(8,128)}, f32[256,256]{1,0:T(8,128)}, f32[256,256]{1,0:T(8,128)}) async-done(((f32[256,256]{1,0:T(8,128)}, f32[256,256]{1,0:T(8,128)}, f32[256,256]{1,0:T(8,128)}, f32[256,256]{1,0:T(8,128)}), (f32[256,256]{1,0:T(8,128)}, f32[256,256]{1,0:T(8,128)}, f32[256,256]{1,0:T(8,128)}, ...) | async-done | bytes 1048592 | tf_op jit(solution)/shard_map/psum | solution.py:153
  432.1 11.8 %psum.78 = f32[256]{0:T(256)S(1)} all-reduce(f32[256]{0:T(256)S(1)} %get-tuple-element.211), channel_id=1, replica_groups=mesh['tm'=4,'ent'=2,'batch'=4] {'ent','batch'}, use_global_device_ids=true, to_apply=%region_14.15 | all-reduce | flops 256 | bytes 2048 | tf_op jit(solution)/shard_map/psum | solution.py:153
  443.9 12.7 %psum.79 = f32[256]{0:T(256)} all-reduce(f32[256]{0:T(256)S(1)} %psum.78), channel_id=1, replica_groups=mesh['tm'=4,'ent'=2,'batch'=4] {'tm'}, use_global_device_ids=true, to_apply=%region_15.16 | all-reduce | flops 256 | bytes 2048 | tf_op jit(solution)/shard_map/psum | solution.py:153
  456.7 29.5 %all-reduce.7.cloned.1.call-done = (f32[256,256]{1,0:T(8,128)}, f32[256,256]{1,0:T(8,128)}, f32[256,256]{1,0:T(8,128)}, f32[256,256]{1,0:T(8,128)}) async-done(((f32[256,256]{1,0:T(8,128)}, f32[256,256]{1,0:T(8,128)}, f32[256,256]{1,0:T(8,128)}, f32[256,256]{1,0:T(8,128)}), (f32[256,256]{1,0:T(8,128)}, f32[256,256]{1,0:T(8,128)}, f32[256,256]{1,0:T(8,128)}, ...) | async-done | bytes 1048592 | tf_op jit(solution)/shard_map/psum | solution.py:153
  486.1 1.7 copy.79
  487.8 1.7 copy.80
  489.5 1.7 copy.81
  491.1 1.7 copy.82
  (130 shorter events, 24.7 us)
Async XLA Ops:
  7.2 35.0 %copy-start = (f32[256,256]{1,0:T(8,128)S(1)}, f32[256,256]{1,0:T(8,128)}, u32[]{:S(2)}) copy-start(f32[256,256]{1,0:T(8,128)} %param.17) | copy-start | bytes 786436
  7.2 2.3 copy-start.1
  7.2 33.4 %reduce-scatter.5.cloned.1.call-start = ((), (), s32[]{:S(2)}) async-start(), calls=%async_computation.4 | async-start | bytes 1572864 | tf_op jit(solution)/shard_map/while/body/eval_jaxpr/reduce_scatter | solution.py:71
  9.2 3.2 copy-start.37
  9.2 3.2 copy-start.42
  9.2 3.4 copy-start.41
  9.4 3.1 copy-start.38
  16.1 1.2 copy-start.14
  16.2 1.4 copy-start.24
  16.2 1.3 copy-start.43
  17.3 23.3 %copy-start.9 = (f32[256,256]{1,0:T(8,128)S(1)}, f32[256,256]{1,0:T(8,128)}, u32[]{:S(2)}) copy-start(f32[256,256]{1,0:T(8,128)} %param.16) | copy-start | bytes 786436
  17.3 77.1 %reduce-scatter.7.cloned.1.call-start = ((), (), s32[]{:S(2)}) async-start(), calls=%async_computation.5 | async-start | bytes 1572864 | tf_op jit(solution)/shard_map/while/body/eval_jaxpr/reduce_scatter | solution.py:71
  44.7 14.7 %collective-permute-start = (f32[512,256]{1,0:T(8,128)}, f32[512,256]{1,0:T(8,128)}, u32[]{:S(2)}, u32[]{:S(2)}) collective-permute-start(f32[512,256]{1,0:T(8,128)} %fusion.45), channel_id=1, source_target_pairs={{0,8},{8,16},{16,24},{1,9},{9,17},{17,25},{2,10},{10,18},{18,26},{... | collective-permute-start | bytes 1572872 | tf_op jit(solution)/shard_map/ppermute | solution.py:12
  59.4 0.8 copy-start.21
  71.9 74.6 %reduce-scatter.9.cloned.1.call-start = ((), (), s32[]{:S(2)}) async-start(), calls=%async_computation.6 | async-start | bytes 1572864 | tf_op jit(solution)/shard_map/while/body/eval_jaxpr/reduce_scatter | solution.py:71
  98.0 14.4 %collective-permute-start.1 = (f32[512,256]{1,0:T(8,128)S(1)}, f32[512,256]{1,0:T(8,128)S(1)}, u32[]{:S(2)}, u32[]{:S(2)}) collective-permute-start(f32[512,256]{1,0:T(8,128)S(1)} %fusion.38), channel_id=1, source_target_pairs={{0,8},{8,16},{16,24},{1,9},{9,17},{17,25},{2,10},{10,18},{18,26},{... | collective-permute-start | bytes 1572872 | tf_op jit(solution)/shard_map/ppermute | solution.py:12
  112.5 0.8 copy-start.22
  113.3 6.8 %copy-start.39 = (f32[2,512]{0,1:T(8,128)S(1)}, f32[2,512]{0,1:T(8,128)}, u32[]{:S(2)}) copy-start(f32[2,512]{0,1:T(8,128)} %copy-done.38) | copy-start | bytes 12292
  123.8 1.2 copy-start.23
  124.9 72.6 %reduce-scatter.11.cloned.1.call-start = ((), (), s32[]{:S(2)}) async-start(), calls=%async_computation.7 | async-start | bytes 1572864 | tf_op jit(solution)/shard_map/while/body/eval_jaxpr/reduce_scatter | solution.py:71
  146.5 17.8 %copy-start.15 = (f32[1,512,256]{2,1,0:T(8,128)S(1)}, f32[1,512,256]{2,1,0:T(8,128)}, u32[]{:S(2)}) copy-start(f32[1,512,256]{2,1,0:T(8,128)} %param.10) | copy-start | bytes 1572868
  149.8 14.4 %collective-permute-start.2 = (f32[512,256]{1,0:T(8,128)S(1)}, f32[512,256]{1,0:T(8,128)S(1)}, u32[]{:S(2)}, u32[]{:S(2)}) collective-permute-start(f32[512,256]{1,0:T(8,128)S(1)} %fusion.31), channel_id=1, source_target_pairs={{0,8},{8,16},{16,24},{1,9},{9,17},{17,25},{2,10},{10,18},{18,26},{... | collective-permute-start | bytes 1572872 | tf_op jit(solution)/shard_map/ppermute | solution.py:12
  164.3 11.7 %copy-start.3 = (f32[512,256]{1,0:T(8,128)}, f32[512,256]{1,0:T(8,128)S(1)}, u32[]{:S(2)}) copy-start(f32[512,256]{1,0:T(8,128)S(1)} %bitcast_select_fusion.2) | copy-start | bytes 1572868
  164.3 6.8 %copy-start.40 = (f32[2,512]{0,1:T(8,128)S(1)}, f32[2,512]{0,1:T(8,128)}, u32[]{:S(2)}) copy-start(f32[2,512]{0,1:T(8,128)} %copy-done.38) | copy-start | bytes 12292
  175.9 49.6 %all-gather.9.cloned.1.call-start = ((), (), s32[]{:S(2)}) async-start(), calls=%async_computation.8 | async-start | bytes 1572864 | tf_op jit(solution)/shard_map/while/body/eval_jaxpr/all_gather | solution.py:76
  177.5 25.1 %copy-start.2 = (f32[1,1,512,256]{3,2,1,0:T(8,128)S(1)}, f32[1,1,512,256]{3,2,1,0:T(8,128)}, u32[]{:S(2)}) copy-start(f32[1,1,512,256]{3,2,1,0:T(8,128)} %param.14) | copy-start | bytes 1572868
  197.5 5.2 %copy-start.10 = (f32[256,256]{1,0:T(8,128)S(1)}, f32[256,256]{1,0:T(8,128)}, u32[]{:S(2)}) copy-start(f32[256,256]{1,0:T(8,128)} %param.16) | copy-start | bytes 786436
  201.8 0.8 copy-start.5
  204.1 69.2 %all-gather.11.cloned.1.call-start = ((), (), s32[]{:S(2)}) async-start(), calls=%async_computation.9 | async-start | bytes 1572864 | tf_op jit(solution)/shard_map/while/body/eval_jaxpr/all_gather | solution.py:76
  230.0 3.5 copy-start.16
  230.0 3.5 copy-start.25
  230.0 3.5 copy-start.36
  233.5 16.2 %copy-start.6 = (f32[512,256]{1,0:T(8,128)S(1)}, f32[512,256]{1,0:T(8,128)}, u32[]{:S(2)}) copy-start(f32[512,256]{1,0:T(8,128)} %copy-done.5) | copy-start | bytes 1572868
  234.2 17.1 %copy-start.11 = (f32[256,256]{1,0:T(8,128)S(1)}, f32[256,256]{1,0:T(8,128)}, u32[]{:S(2)}) copy-start(f32[256,256]{1,0:T(8,128)} %param.16) | copy-start | bytes 786436
  234.2 15.5 %collective-permute-start.3 = (f32[512,256]{1,0:T(8,128)S(1)}, f32[512,256]{1,0:T(8,128)S(1)}, u32[]{:S(2)}, u32[]{:S(2)}) collective-permute-start(f32[512,256]{1,0:T(8,128)S(1)} %fusion.23), channel_id=1, source_target_pairs={{8,0},{16,8},{24,16},{9,1},{17,9},{25,17},{10,2},{18,10},{26,18},{... | collective-permute-start | bytes 1572872 | tf_op jit(solution)/shard_map/ppermute | solution.py:12
  249.8 0.8 copy-start.28
  250.6 0.8 copy-start.19
  252.8 68.4 %all-gather.13.cloned.1.call-start = ((), (), s32[]{:S(2)}) async-start(), calls=%async_computation.10 | async-start | bytes 1572864 | tf_op jit(solution)/shard_map/while/body/eval_jaxpr/all_gather | solution.py:76
  277.8 3.5 copy-start.17
  277.8 3.5 copy-start.26
  277.8 3.5 copy-start.29
  277.8 3.5 copy-start.33
  281.4 16.3 %copy-start.7 = (f32[512,256]{1,0:T(8,128)S(1)}, f32[512,256]{1,0:T(8,128)}, u32[]{:S(2)}) copy-start(f32[512,256]{1,0:T(8,128)} %copy-done.5) | copy-start | bytes 1572868
  282.1 17.2 %copy-start.12 = (f32[256,256]{1,0:T(8,128)S(1)}, f32[256,256]{1,0:T(8,128)}, u32[]{:S(2)}) copy-start(f32[256,256]{1,0:T(8,128)} %param.16) | copy-start | bytes 786436
  282.1 15.5 %collective-permute-start.4 = (f32[512,256]{1,0:T(8,128)S(1)}, f32[512,256]{1,0:T(8,128)S(1)}, u32[]{:S(2)}, u32[]{:S(2)}) collective-permute-start(f32[512,256]{1,0:T(8,128)S(1)} %add_add_fusion.1), channel_id=1, source_target_pairs={{8,0},{16,8},{24,16},{9,1},{17,9},{25,17},{10,2},{18,10},{26,18},{... | collective-permute-start | bytes 1572872 | tf_op jit(solution)/shard_map/ppermute | solution.py:12
  297.7 0.8 copy-start.30
  298.5 0.8 copy-start.20
  300.7 68.0 %all-gather.15.cloned.1.call-start = ((), (), s32[]{:S(2)}) async-start(), calls=%async_computation.11 | async-start | bytes 1572864 | tf_op jit(solution)/shard_map/while/body/eval_jaxpr/all_gather | solution.py:76
  325.7 3.5 copy-start.18
  325.7 3.5 copy-start.27
  325.7 3.5 copy-start.31
  325.7 3.5 copy-start.34
  329.2 16.3 %copy-start.4 = (f32[512,256]{1,0:T(8,128)S(1)}, f32[512,256]{1,0:T(8,128)}, u32[]{:S(2)}) copy-start(f32[512,256]{1,0:T(8,128)} %copy-done.3) | copy-start | bytes 1572868
  329.3 16.3 %copy-start.8 = (f32[512,256]{1,0:T(8,128)S(1)}, f32[512,256]{1,0:T(8,128)}, u32[]{:S(2)}) copy-start(f32[512,256]{1,0:T(8,128)} %copy-done.5) | copy-start | bytes 1572868
  330.0 16.7 %copy-start.13 = (f32[256,256]{1,0:T(8,128)S(1)}, f32[256,256]{1,0:T(8,128)}, u32[]{:S(2)}) copy-start(f32[256,256]{1,0:T(8,128)} %param.16) | copy-start | bytes 786436
  330.0 15.5 %collective-permute-start.5 = (f32[512,256]{1,0:T(8,128)S(1)}, f32[512,256]{1,0:T(8,128)S(1)}, u32[]{:S(2)}, u32[]{:S(2)}) collective-permute-start(f32[512,256]{1,0:T(8,128)S(1)} %add_add_fusion), channel_id=1, source_target_pairs={{8,0},{16,8},{24,16},{9,1},{17,9},{25,17},{10,2},{18,10},{26,18},{... | collective-permute-start | bytes 1572872 | tf_op jit(solution)/shard_map/ppermute | solution.py:12
  346.8 3.5 copy-start.32
  346.8 5.2 %copy-start.35 = (f32[1,512,256]{2,1,0:T(8,128)S(1)}, f32[1,512,256]{2,1,0:T(8,128)}, u32[]{:S(2)}) copy-start(f32[1,512,256]{2,1,0:T(8,128)} %reduce-scatter.11.cloned.1.call-done) | copy-start | bytes 1572868
  348.2 83.9 %all-reduce.5.cloned.1.call-start = ((), (), s32[]{:S(2)}) async-start(), calls=%async_computation.12 | async-start | bytes 2097152 | tf_op jit(solution)/shard_map/psum | solution.py:153
  375.0 111.1 %all-reduce.7.cloned.1.call-start = ((), (), s32[]{:S(2)}) async-start(), calls=%async_computation.13 | async-start | bytes 2097152 | tf_op jit(solution)/shard_map/psum | solution.py:153
Sparse Core Ops, SparseCore 0:
  17.4 23.1 reduce-scatter.4
  72.0 22.3 reduce-scatter.6
  125.0 21.3 reduce-scatter.8
  176.0 21.3 reduce-scatter.10
  204.2 21.2 all-gather.8
  252.9 20.3 all-gather.10
  300.8 20.3 all-gather.12
  348.3 20.3 all-gather.14
  375.1 56.9 all-reduce.4
  434.5 51.5 all-reduce.6
